TPU v7x, 256 devices: a whole 4x4x8 slice. The times are simulated.
256 devices in a mesh: xy: 64 (over z_hi, y, x, core), gz: 4 (over z_lo).
Axes of the slice: x: 4, y: 4, z: 8 (z_hi: 2, z_lo: 4; z = z_hi * 4 + z_lo), core: 2. Of those that a mesh axis runs over, the one named last changes fastest.
Arguments:
- field: float32 [64, 2, 3, 512, 256], P('gz', None, None, 'xy'), may hold values from -6 to 6
- source: float32 [64, 2, 3, 512, 256], P('gz', None, None, 'xy'), may hold values from -6 to 6
- classes: int32 [64, 512, 256], P('gz', 'xy'), may hold values from 0 to 15
- boundary: int32 [64, 512, 256], P('gz', 'xy'), may hold values 0 or 1
- conductance: float32 [16], replicated, may hold values from 0.001 to 1
- angles: float32 [3], replicated, may hold values from -3.140625 to 3.140625
- strengths: float32 [3], replicated, may hold values from 0.5 to 2
Outputs:
- relaxed: float32 [64, 2, 3, 512, 256], P('gz', None, None, 'xy')
All inputs are finite; a program needn't handle non-finite values. No bound on the sum of `boundary` on one device may be relied on, other than what follows from the above.
Results may differ from a plain program's by a relative error of at most 0.00029.
Values sent between devices are 32-bit elements; how exact they have to be, the bound alone decides.
A program may use at most 64 MiB of HBM per device.

v0:
```python
import functools

import jax
import jax.numpy as jnp
from jax import lax
from jax.experimental import pallas as pl
from jax.experimental.pallas import tpu as pltpu
from jax.sharding import PartitionSpec as P

SWEEPS = 2
COUPLING = 0.1
PENALTY = 4.0
CHUNKS = 4
MESH = pl.DeviceIdType.MESH


def mul(left, right):
    return (left[0] * right[0] - left[1] * right[1], left[0] * right[1] + left[1] * right[0])


def add(left, right):
    return (left[0] + right[0], left[1] + right[1])


def inverse(value):
    weight = 1.0 / (value[0] * value[0] + value[1] * value[1])
    return (value[0] * weight, -(value[1] * weight))


def one_less(value):
    return (1.0 - value[0], -value[1])


def get(ref, *index):
    return (ref[(*index, 0)], ref[(*index, 1)])


def put(ref, value, *index):
    ref[(*index, 0)] = value[0]
    ref[(*index, 1)] = value[1]


def look_up(table_ref, count, index):
    values = [table_ref[c] for c in range(count)]
    bit = 1
    while len(values) > 1:
        odd = (index & bit) != 0
        values = [
            jnp.where(odd, values[n + 1], values[n]) if n + 1 < len(values) else values[n]
            for n in range(0, len(values), 2)
        ]
        bit *= 2
    return values[0]


def rotation(angles_ref):
    turns = [jnp.full((8, 128), angles_ref[n], jnp.float32) for n in range(3)]
    c0, c1, c2 = [jnp.cos(t)[0, 0] for t in turns]
    s0, s1, s2 = [jnp.sin(t)[0, 0] for t in turns]
    first = [[c0 * c1, -s0, c0 * s1], [s0 * c1, c0, s0 * s1], [-s1, jnp.float32(0.0), c1]]
    return [[f[0] * c2 + f[1] * s2, f[1] * c2 - f[0] * s2, f[2]] for f in first]


def kernel(
    ni, nk,
    field, source, classes, boundary, conductance, angles, strengths,
    out,
    cur, src, cls, bnd, piv, vec_v, vec_u, sol,
    ends, coef_r, coef_c,
    halo_out, halo_in, chain_out, chain_in,
    load_sem, halo_send, halo_recv, chain_send, chain_recv,
):
    i = lax.axis_index("xy")
    k = lax.axis_index("gz")
    depth, _, comps, rows, lanes = cur.shape
    per = depth // CHUNKS
    last = depth - 1

    loads = [
        pltpu.make_async_copy(a, b, load_sem.at[n])
        for n, (a, b) in enumerate(((field, cur), (classes, cls), (boundary, bnd), (source, src)))
    ]
    for copy in loads:
        copy.start()

    barrier = pltpu.get_barrier_semaphore()
    neighbours = (
        (i > 0, {"xy": i - 1}),
        (i < ni - 1, {"xy": i + 1}),
        (k > 0, {"gz": k - 1}),
        (k < nk - 1, {"gz": k + 1}),
    )
    for there, target in neighbours:
        @pl.when(there)
        def _():
            pl.semaphore_signal(barrier, inc=1, device_id=target, device_id_type=MESH)

    @pl.when(i == 0)
    def _():
        for n in range(SWEEPS):
            halo_in[n, 0] = jnp.zeros(halo_in.shape[2:], jnp.float32)

    @pl.when(i == ni - 1)
    def _():
        for n in range(SWEEPS):
            halo_in[n, 1] = jnp.zeros(halo_in.shape[2:], jnp.float32)

    @pl.when(k == 0)
    def _():
        for n in range(SWEEPS + 1):
            chain_in[n, 0] = jnp.zeros(chain_in.shape[2:], jnp.float32)

    @pl.when(k == nk - 1)
    def _():
        for n in range(SWEEPS + 1):
            chain_in[n, 1] = jnp.zeros(chain_in.shape[2:], jnp.float32)

    turn = rotation(angles)

    def halo_copy(number, side, chunk):
        part = pl.ds(chunk * per, per)
        return pltpu.make_async_remote_copy(
            src_ref=halo_out.at[number, side, part],
            dst_ref=halo_in.at[number, 1 - side, part],
            send_sem=halo_send.at[number, side, chunk],
            recv_sem=halo_recv.at[number, 1 - side, chunk],
            device_id={"xy": i + 2 * side - 1},
            device_id_type=MESH,
        )

    sides = ((0, i > 0), (1, i < ni - 1))

    def send_halo(number, chunk):
        for side, there in sides:
            @pl.when(there)
            def _():
                halo_copy(number, side, chunk).start()

    def wait_halo(number):
        for side, there in sides:
            @pl.when(there)
            def _():
                for chunk in range(CHUNKS):
                    halo_copy(number, 1 - side, chunk).wait_recv()

    def finish_halo(number):
        for side, there in sides:
            @pl.when(there)
            def _():
                for chunk in range(CHUNKS):
                    halo_copy(number, side, chunk).wait_send()

    def chain_copy(stage, way, comp):
        return pltpu.make_async_remote_copy(
            src_ref=chain_out.at[stage, way, comp],
            dst_ref=chain_in.at[stage, way, comp],
            send_sem=chain_send.at[stage, way, comp],
            recv_sem=chain_recv.at[stage, way, comp],
            device_id={"gz": k + 1 - 2 * way},
            device_id_type=MESH,
        )

    def run_chain(stage, step):
        near_half = lax.div(k * 2, nk)
        for order in range(2):
            way = near_half if order == 0 else 1 - near_half
            has_in = jnp.where(way == 0, k, nk - 1 - k) > 0
            has_out = jnp.where(way == 0, nk - 1 - k, k) > 0
            for comp in range(comps):
                @pl.when(has_in)
                def _():
                    chain_copy(stage, way, comp).wait_recv()

                put(chain_out, step(way, comp, get(chain_in, stage, way, comp)), stage, way, comp)

                @pl.when(has_out)
                def _():
                    chain_copy(stage, way, comp).start()

    def finish_chain(stage):
        for way, there in ((0, k < nk - 1), (1, k > 0)):
            @pl.when(there)
            def _():
                for comp in range(comps):
                    chain_copy(stage, way, comp).wait_send()

    pl.semaphore_wait(barrier, sum(there.astype(jnp.int32) for there, _ in neighbours))

    loads[0].wait()
    for chunk in range(CHUNKS):
        for z in range(chunk * per, (chunk + 1) * per):
            for part in range(2):
                here = cur[z, part]
                halo_out[0, 0, z, part] = here[:, :1]
                halo_out[0, 1, z, part] = here[:, rows - 1:]
        send_halo(0, chunk)

    loads[1].wait()
    loads[2].wait()
    for z in range(depth):
        sigma = look_up(conductance, conductance.shape[0], cls[z])
        real = (2.0 + 4.0 * COUPLING) + PENALTY * bnd[z].astype(jnp.float32)
        for comp in range(comps):
            diagonal = (real, sigma * strengths[comp])
            if z:
                before = get(piv, z - 1, comp)
                diagonal = (diagonal[0] - before[0], diagonal[1] - before[1])
            pivot = inverse(diagonal)
            put(piv, pivot, z, comp)
            if z == 1:
                put(vec_v, before, z, comp)
            elif z > 1:
                put(vec_v, mul(before, get(vec_v, z - 1, comp)), z, comp)
    for comp in range(comps):
        pivot = get(piv, last, comp)
        column_v, column_u = mul(pivot, get(vec_v, last, comp)), pivot
        put(vec_v, column_v, last, comp)
        put(vec_u, column_u, last, comp)
        put(ends, column_u, 1, comp)
        for z in range(last - 1, -1, -1):
            pivot = get(piv, z, comp)
            column_u = mul(pivot, column_u)
            put(vec_u, column_u, z, comp)
            if z:
                column_v = mul(pivot, add(get(vec_v, z, comp), column_v))
            else:
                column_v = mul(pivot, (1.0 + column_v[0], column_v[1]))
            put(vec_v, column_v, z, comp)
        put(ends, column_v, 0, comp)

    def coefficient_step(way, comp, arrived):
        near, far = get(ends, way, comp), get(ends, 1 - way, comp)
        across = get(vec_u, 0, comp)
        passed = mul(across, inverse(one_less(mul(near, arrived))))
        put(coef_c, passed, way, comp)
        linked = mul(passed, arrived)
        put(coef_r, linked, way, comp)
        return add(far, mul(linked, across))

    run_chain(0, coefficient_step)

    loads[3].wait()
    sublane = lax.broadcasted_iota(jnp.int32, (comps, rows, lanes), 1)
    lane = lax.broadcasted_iota(jnp.int32, (comps, rows, lanes), 2)

    for number in range(SWEEPS):
        stage = number + 1
        wait_halo(number)
        carried = None
        for z in range(depth):
            turned = []
            for part in range(2):
                here = cur[z, part]
                up = jnp.where(sublane == 0, halo_in[number, 0, z, part], pltpu.roll(here, 1, 1))
                down = jnp.where(
                    sublane == rows - 1, halo_in[number, 1, z, part], pltpu.roll(here, rows - 1, 1)
                )
                left = jnp.where(lane == 0, 0.0, pltpu.roll(here, 1, 2))
                right = jnp.where(lane == lanes - 1, 0.0, pltpu.roll(here, lanes - 1, 2))
                driven = src[z, part] + COUPLING * ((down + up) + (right + left))
                turned.append([
                    turn[0][j] * driven[0] + turn[1][j] * driven[1] + turn[2][j] * driven[2]
                    for j in range(comps)
                ])
            for comp in range(comps):
                forcing = (turned[0][comp], turned[1][comp])
                if z:
                    forcing = add(forcing, mul(get(piv, z - 1, comp), get(sol, z - 1, comp)))
                put(sol, forcing, z, comp)
        for comp in range(comps):
            value = mul(get(piv, last, comp), get(sol, last, comp))
            put(sol, value, last, comp)
            for z in range(last - 1, -1, -1):
                value = mul(get(piv, z, comp), add(get(sol, z, comp), value))
                put(sol, value, z, comp)

        def forcing_step(way, comp, arrived):
            near = get(sol, last * way, comp)
            far = get(sol, last * (1 - way), comp)
            local = add(far, mul(get(coef_r, way, comp), near))
            return add(local, mul(get(coef_c, way, comp), arrived))

        run_chain(stage, forcing_step)

        first_in, last_in = [], []
        for comp in range(comps):
            p_in, q_in = get(chain_in, 0, 0, comp), get(chain_in, 0, 1, comp)
            p_out, q_out = get(chain_out, 0, 0, comp), get(chain_out, 0, 1, comp)
            above = add(get(chain_in, stage, 0, comp), mul(p_in, get(chain_out, stage, 1, comp)))
            below = add(get(chain_in, stage, 1, comp), mul(q_in, get(chain_out, stage, 0, comp)))
            first_in.append(mul(above, inverse(one_less(mul(q_out, p_in)))))
            last_in.append(mul(below, inverse(one_less(mul(p_out, q_in)))))
        for chunk in range(CHUNKS):
            for z in range(chunk * per, (chunk + 1) * per):
                solved = []
                for comp in range(comps):
                    value = add(
                        mul(get(vec_v, z, comp), first_in[comp]),
                        mul(get(vec_u, z, comp), last_in[comp]),
                    )
                    solved.append(add(get(sol, z, comp), value))
                for part in range(2):
                    for c in range(comps):
                        value = (
                            turn[c][0] * solved[0][part]
                            + turn[c][1] * solved[1][part]
                            + turn[c][2] * solved[2][part]
                        )
                        if stage == SWEEPS:
                            out[z, part, c] = value
                        else:
                            cur[z, part, c] = value
                            halo_out[stage, 0, z, part, c] = value[:1]
                            halo_out[stage, 1, z, part, c] = value[rows - 1:]
            if stage < SWEEPS:
                send_halo(stage, chunk)

    for number in range(SWEEPS):
        finish_halo(number)
    for stage in range(SWEEPS + 1):
        finish_chain(stage)


def local(ni, nk, field, source, classes, boundary, conductance, angles, strengths):
    depth, _, comps, rows, lanes = field.shape
    block = (depth, 2, comps, rows, lanes)
    lines = (depth, comps, 2, rows, lanes)
    ends = (2, comps, 2, rows, lanes)
    vmem = lambda *shape: pltpu.VMEM(shape, jnp.float32)
    dma = lambda *shape: pltpu.SemaphoreType.DMA(shape)
    whole = pl.BlockSpec(memory_space=pltpu.HBM)
    scalars = pl.BlockSpec(memory_space=pltpu.SMEM)
    return pl.pallas_call(
        functools.partial(kernel, ni, nk),
        out_shape=jax.ShapeDtypeStruct(block, jnp.float32),
        in_specs=[whole] * 4 + [scalars] * 3,
        out_specs=pl.BlockSpec(memory_space=pltpu.VMEM),
        scratch_shapes=[
            vmem(*block), vmem(*block),
            pltpu.VMEM(classes.shape, jnp.int32), pltpu.VMEM(boundary.shape, jnp.int32),
            vmem(*lines), vmem(*lines), vmem(*lines), vmem(*lines),
            vmem(*ends), vmem(*ends), vmem(*ends),
            vmem(SWEEPS, 2, depth, 2, comps, 1, lanes), vmem(SWEEPS, 2, depth, 2, comps, 1, lanes),
            vmem(SWEEPS + 1, *ends), vmem(SWEEPS + 1, *ends),
            dma(4), dma(SWEEPS, 2, CHUNKS), dma(SWEEPS, 2, CHUNKS),
            dma(SWEEPS + 1, 2, comps), dma(SWEEPS + 1, 2, comps),
        ],
        compiler_params=pltpu.CompilerParams(
            collective_id=0, has_side_effects=True, vmem_limit_bytes=67043328
        ),
    )(field, source, classes, boundary, conductance, angles, strengths)


def solution(mesh):
    in_specs = (
        P("gz", None, None, "xy", None),
        P("gz", None, None, "xy", None),
        P("gz", "xy", None),
        P("gz", "xy", None),
        P(),
        P(),
        P(),
    )
    out_specs = P("gz", None, None, "xy", None)
    body = functools.partial(local, mesh.shape["xy"], mesh.shape["gz"])
    return jax.shard_map(body, mesh=mesh, in_specs=in_specs, out_specs=out_specs, check_vma=False)
```

profile of v0, /device:TPU:31, one launch (start us, length us, event | category | flops | bytes accessed | tf_op | source)
XLA Modules:
  0.0 45.4 jit_solution(1376812807107643630)
XLA Ops:
  0.0 43.4 %shard_map.73 = f32[16,2,3,8,256]{4,3,2,1,0:T(8,128)} custom-call(f32[16,2,3,8,256]{4,3,2,1,0:T(8,128)} %field.1, f32[16,2,3,8,256]{4,3,2,1,0:T(8,128)} %source.1, s32[16,8,256]{2,1,0:T(8,128)} %classes.1, s32[16,8,256]{2,1,0:T(8,128)} %boundary.1, f32[16]{0:T(128)} %conductance.1, f32[3]{0:T(128)} %angles.1, f32[3]{0:T(128)} %strengths.1), custom_call_target="tpu_custom_call" | custom-call | tf_op jit(solution)/shard_map/pallas_call | solution.py:333
  43.4 2.1 %copy.9 = f32[16,2,3,8,256]{4,3,2,1,0:T(8,128)} copy(f32[16,2,3,8,256]{4,3,2,1,0:T(8,128)} %shard_map.73) | data formatting | bytes 1572864
where the time goes:
time: 45.6 us; the launch traced here: 45.4 us
  Pallas kernels  43.4 us (95%)
  local copies, waits for them, and re-layouts  2.06 us (5%)
    pallas_call x1, Pallas kernels, local(): pl.pallas_call(functools.partial(kernel, ni, nk), out_shape=jax.ShapeDtyp...  43.4 us
    unnamed x1, local copies, waits for them, and re-layouts  2.06 us

commit v1 on v0

--- a/solution.py
+++ b/solution.py
@@ -65,10 +65,10 @@
     ni, nk,
     field, source, classes, boundary, conductance, angles, strengths,
     out,
-    cur, src, cls, bnd, piv, vec_v, vec_u, sol,
+    cur, src, cls, bnd, piv, vec_v, vec_u, rhs, sol,
     ends, coef_r, coef_c,
-    halo_out, halo_in, chain_out, chain_in,
-    load_sem, halo_send, halo_recv, chain_send, chain_recv,
+    halo_out, halo_in, chain_out, chain_in, edge_out, edge_in,
+    load_sem, halo_send, halo_recv, chain_send, chain_recv, edge_send, edge_recv,
 ):
     i = lax.axis_index("xy")
     k = lax.axis_index("gz")
@@ -84,36 +84,31 @@
         copy.start()
 
     barrier = pltpu.get_barrier_semaphore()
-    neighbours = (
-        (i > 0, {"xy": i - 1}),
-        (i < ni - 1, {"xy": i + 1}),
-        (k > 0, {"gz": k - 1}),
-        (k < nk - 1, {"gz": k + 1}),
-    )
+    neighbours = [(i > 0, {"xy": i - 1}), (i < ni - 1, {"xy": i + 1})]
+    for far in range(1, nk):
+        neighbours += [(k >= far, {"gz": k - far}), (k < nk - far, {"gz": k + far})]
     for there, target in neighbours:
         @pl.when(there)
         def _():
             pl.semaphore_signal(barrier, inc=1, device_id=target, device_id_type=MESH)
 
-    @pl.when(i == 0)
-    def _():
-        for n in range(SWEEPS):
-            halo_in[n, 0] = jnp.zeros(halo_in.shape[2:], jnp.float32)
-
-    @pl.when(i == ni - 1)
-    def _():
-        for n in range(SWEEPS):
-            halo_in[n, 1] = jnp.zeros(halo_in.shape[2:], jnp.float32)
-
-    @pl.when(k == 0)
-    def _():
-        for n in range(SWEEPS + 1):
-            chain_in[n, 0] = jnp.zeros(chain_in.shape[2:], jnp.float32)
-
-    @pl.when(k == nk - 1)
-    def _():
-        for n in range(SWEEPS + 1):
-            chain_in[n, 1] = jnp.zeros(chain_in.shape[2:], jnp.float32)
+    for side, alone in ((0, i == 0), (1, i == ni - 1)):
+        @pl.when(alone)
+        def _():
+            for n in range(SWEEPS):
+                halo_in[n, side] = jnp.zeros(halo_in.shape[2:], jnp.float32)
+
+    for way, place in ((0, k), (1, nk - 1 - k)):
+        @pl.when(place == 0)
+        def _():
+            for n in range(SWEEPS + 1):
+                chain_in[n, way] = jnp.zeros(chain_in.shape[2:], jnp.float32)
+
+        for far in range(1, nk):
+            @pl.when(place < far)
+            def _():
+                for n in range(SWEEPS + 1):
+                    edge_in[n, way, far - 1] = jnp.zeros(edge_in.shape[3:], jnp.float32)
 
     turn = rotation(angles)
 
@@ -150,6 +145,9 @@
                 for chunk in range(CHUNKS):
                     halo_copy(number, side, chunk).wait_send()
 
+    def place_of(way):
+        return jnp.where(way == 0, k, nk - 1 - k)
+
     def chain_copy(stage, way, comp):
         return pltpu.make_async_remote_copy(
             src_ref=chain_out.at[stage, way, comp],
@@ -160,22 +158,17 @@
             device_id_type=MESH,
         )
 
-    def run_chain(stage, step):
-        near_half = lax.div(k * 2, nk)
-        for order in range(2):
-            way = near_half if order == 0 else 1 - near_half
-            has_in = jnp.where(way == 0, k, nk - 1 - k) > 0
-            has_out = jnp.where(way == 0, nk - 1 - k, k) > 0
-            for comp in range(comps):
-                @pl.when(has_in)
-                def _():
-                    chain_copy(stage, way, comp).wait_recv()
-
-                put(chain_out, step(way, comp, get(chain_in, stage, way, comp)), stage, way, comp)
-
-                @pl.when(has_out)
-                def _():
-                    chain_copy(stage, way, comp).start()
+    def relay(stage, way, step):
+        for comp in range(comps):
+            @pl.when(place_of(way) > 0)
+            def _():
+                chain_copy(stage, way, comp).wait_recv()
+
+            put(chain_out, step(way, comp, get(chain_in, stage, way, comp)), stage, way, comp)
+
+            @pl.when(place_of(way) < nk - 1)
+            def _():
+                chain_copy(stage, way, comp).start()
 
     def finish_chain(stage):
         for way, there in ((0, k < nk - 1), (1, k > 0)):
@@ -184,16 +177,46 @@
                 for comp in range(comps):
                     chain_copy(stage, way, comp).wait_send()
 
-    pl.semaphore_wait(barrier, sum(there.astype(jnp.int32) for there, _ in neighbours))
+    def edge_copy(stage, way, far):
+        return pltpu.make_async_remote_copy(
+            src_ref=edge_out.at[stage, way],
+            dst_ref=edge_in.at[stage, way, far - 1],
+            send_sem=edge_send.at[stage, way, far - 1],
+            recv_sem=edge_recv.at[stage, way, far - 1],
+            device_id={"gz": k + far * (1 - 2 * way)},
+            device_id_type=MESH,
+        )
+
+    def send_edges(stage, way, values):
+        for comp in range(comps):
+            for part in range(2):
+                edge_out[stage, way, comp, part, :1] = values[comp][part][:1]
+                edge_out[stage, way, comp, part, 1:] = values[comp][part][rows - 1:]
+        for far in range(nk - 1, 0, -1):
+            @pl.when(place_of(way) < nk - far)
+            def _():
+                edge_copy(stage, way, far).start()
+
+    def wait_edges(stage):
+        for way in range(2):
+            for far in range(1, nk):
+                @pl.when(place_of(way) >= far)
+                def _():
+                    edge_copy(stage, way, far).wait_recv()
+
+    def finish_edges(stage):
+        for way in range(2):
+            for far in range(1, nk):
+                @pl.when(place_of(way) < nk - far)
+                def _():
+                    edge_copy(stage, way, far).wait_send()
 
     loads[0].wait()
-    for chunk in range(CHUNKS):
-        for z in range(chunk * per, (chunk + 1) * per):
-            for part in range(2):
-                here = cur[z, part]
-                halo_out[0, 0, z, part] = here[:, :1]
-                halo_out[0, 1, z, part] = here[:, rows - 1:]
-        send_halo(0, chunk)
+    for z in range(depth):
+        for part in range(2):
+            here = cur[z, part]
+            halo_out[0, 0, z, part] = here[:, :1]
+            halo_out[0, 1, z, part] = here[:, rows - 1:]
 
     loads[1].wait()
     loads[2].wait()
@@ -228,6 +251,10 @@
             put(vec_v, column_v, z, comp)
         put(ends, column_v, 0, comp)
 
+    pl.semaphore_wait(barrier, sum(there.astype(jnp.int32) for there, _ in neighbours))
+    for chunk in range(CHUNKS):
+        send_halo(0, chunk)
+
     def coefficient_step(way, comp, arrived):
         near, far = get(ends, way, comp), get(ends, 1 - way, comp)
         across = get(vec_u, 0, comp)
@@ -237,36 +264,67 @@
         put(coef_r, linked, way, comp)
         return add(far, mul(linked, across))
 
-    run_chain(0, coefficient_step)
-
-    loads[3].wait()
+    def relay_coefficients(way):
+        relay(0, way, coefficient_step)
+        send_edges(0, way, [get(coef_c, way, comp) for comp in range(comps)])
+
+    def local_forcing(way, comp):
+        near = get(sol, last * way, comp)
+        far = get(sol, last * (1 - way), comp)
+        return add(far, mul(get(coef_r, way, comp), near))
+
+    def forcing_step(way, comp, arrived):
+        return add(local_forcing(way, comp), mul(get(coef_c, way, comp), arrived))
+
+    def send_forcing_edges(stage, way):
+        send_edges(stage, way, [local_forcing(way, comp) for comp in range(comps)])
+
     sublane = lax.broadcasted_iota(jnp.int32, (comps, rows, lanes), 1)
     lane = lax.broadcasted_iota(jnp.int32, (comps, rows, lanes), 2)
-
-    for number in range(SWEEPS):
-        stage = number + 1
-        wait_halo(number)
-        carried = None
+    plane = lax.broadcasted_iota(jnp.int32, (rows, lanes), 0)
+
+    def turned_back(vectors):
+        return [
+            turn[0][j] * vectors[0] + turn[1][j] * vectors[1] + turn[2][j] * vectors[2]
+            for j in range(comps)
+        ]
+
+    def without_halo():
         for z in range(depth):
-            turned = []
             for part in range(2):
                 here = cur[z, part]
-                up = jnp.where(sublane == 0, halo_in[number, 0, z, part], pltpu.roll(here, 1, 1))
-                down = jnp.where(
-                    sublane == rows - 1, halo_in[number, 1, z, part], pltpu.roll(here, rows - 1, 1)
-                )
+                up = jnp.where(sublane == 0, 0.0, pltpu.roll(here, 1, 1))
+                down = jnp.where(sublane == rows - 1, 0.0, pltpu.roll(here, rows - 1, 1))
                 left = jnp.where(lane == 0, 0.0, pltpu.roll(here, 1, 2))
                 right = jnp.where(lane == lanes - 1, 0.0, pltpu.roll(here, lanes - 1, 2))
                 driven = src[z, part] + COUPLING * ((down + up) + (right + left))
-                turned.append([
-                    turn[0][j] * driven[0] + turn[1][j] * driven[1] + turn[2][j] * driven[2]
-                    for j in range(comps)
-                ])
-            for comp in range(comps):
-                forcing = (turned[0][comp], turned[1][comp])
-                if z:
-                    forcing = add(forcing, mul(get(piv, z - 1, comp), get(sol, z - 1, comp)))
-                put(sol, forcing, z, comp)
+                for comp, value in enumerate(turned_back(driven)):
+                    rhs[z, comp, part] = value
+            forward(z, [get(rhs, z, comp) for comp in range(comps)])
+        backward()
+
+    def with_halo(number):
+        for z in range(depth):
+            added = []
+            for part in range(2):
+                outer = jnp.where(
+                    sublane == 0,
+                    halo_in[number, 0, z, part],
+                    jnp.where(sublane == rows - 1, halo_in[number, 1, z, part], 0.0),
+                )
+                added.append(turned_back(COUPLING * outer))
+            forward(z, [
+                add(get(rhs, z, comp), (added[0][comp], added[1][comp])) for comp in range(comps)
+            ])
+        backward()
+
+    def forward(z, forcings):
+        for comp, forcing in enumerate(forcings):
+            if z:
+                forcing = add(forcing, mul(get(piv, z - 1, comp), get(sol, z - 1, comp)))
+            put(sol, forcing, z, comp)
+
+    def backward():
         for comp in range(comps):
             value = mul(get(piv, last, comp), get(sol, last, comp))
             put(sol, value, last, comp)
@@ -274,20 +332,59 @@
                 value = mul(get(piv, z, comp), add(get(sol, z, comp), value))
                 put(sol, value, z, comp)
 
-        def forcing_step(way, comp, arrived):
-            near = get(sol, last * way, comp)
-            far = get(sol, last * (1 - way), comp)
-            local = add(far, mul(get(coef_r, way, comp), near))
-            return add(local, mul(get(coef_c, way, comp), arrived))
-
-        run_chain(stage, forcing_step)
-
+    near_way = lax.div(k * 2, nk)
+    far_way = 1 - near_way
+
+    @pl.when(place_of(near_way) == 0)
+    def _():
+        relay_coefficients(near_way)
+
+    loads[3].wait()
+    for number in range(SWEEPS):
+        stage = number + 1
+        without_halo()
+        if number == 0:
+            @pl.when(place_of(near_way) > 0)
+            def _():
+                relay_coefficients(near_way)
+
+        relay(stage, near_way, forcing_step)
+        wait_halo(number)
+        with_halo(number)
+        send_forcing_edges(stage, near_way)
+        if number == 0:
+            relay_coefficients(far_way)
+        send_forcing_edges(stage, far_way)
+        relay(stage, far_way, forcing_step)
+
+        if number == 0:
+            wait_edges(0)
+        wait_edges(stage)
         first_in, last_in = [], []
         for comp in range(comps):
+            arrived, leaving = [], []
+            for way in range(2):
+                total = None
+                for far in range(nk - 1, 0, -1):
+                    term = get(edge_in, stage, way, far - 1, comp)
+                    if total is not None:
+                        term = add(term, mul(get(edge_in, 0, way, far - 1, comp), total))
+                    total = term
+                inner = get(chain_in, stage, way, comp)
+                value = tuple(
+                    jnp.where(
+                        plane == 0,
+                        total[part][:1],
+                        jnp.where(plane == rows - 1, total[part][1:], inner[part]),
+                    )
+                    for part in range(2)
+                )
+                arrived.append(value)
+                leaving.append(forcing_step(way, comp, value))
             p_in, q_in = get(chain_in, 0, 0, comp), get(chain_in, 0, 1, comp)
             p_out, q_out = get(chain_out, 0, 0, comp), get(chain_out, 0, 1, comp)
-            above = add(get(chain_in, stage, 0, comp), mul(p_in, get(chain_out, stage, 1, comp)))
-            below = add(get(chain_in, stage, 1, comp), mul(q_in, get(chain_out, stage, 0, comp)))
+            above = add(arrived[0], mul(p_in, leaving[1]))
+            below = add(arrived[1], mul(q_in, leaving[0]))
             first_in.append(mul(above, inverse(one_less(mul(q_out, p_in)))))
             last_in.append(mul(below, inverse(one_less(mul(p_out, q_in)))))
         for chunk in range(CHUNKS):
@@ -319,6 +416,7 @@
         finish_halo(number)
     for stage in range(SWEEPS + 1):
         finish_chain(stage)
+        finish_edges(stage)
 
 
 def local(ni, nk, field, source, classes, boundary, conductance, angles, strengths):
@@ -338,12 +436,14 @@
         scratch_shapes=[
             vmem(*block), vmem(*block),
             pltpu.VMEM(classes.shape, jnp.int32), pltpu.VMEM(boundary.shape, jnp.int32),
-            vmem(*lines), vmem(*lines), vmem(*lines), vmem(*lines),
+            vmem(*lines), vmem(*lines), vmem(*lines), vmem(*lines), vmem(*lines),
             vmem(*ends), vmem(*ends), vmem(*ends),
             vmem(SWEEPS, 2, depth, 2, comps, 1, lanes), vmem(SWEEPS, 2, depth, 2, comps, 1, lanes),
             vmem(SWEEPS + 1, *ends), vmem(SWEEPS + 1, *ends),
+            vmem(SWEEPS + 1, 2, comps, 2, 2, lanes), vmem(SWEEPS + 1, 2, nk - 1, comps, 2, 2, lanes),
             dma(4), dma(SWEEPS, 2, CHUNKS), dma(SWEEPS, 2, CHUNKS),
             dma(SWEEPS + 1, 2, comps), dma(SWEEPS + 1, 2, comps),
+            dma(SWEEPS + 1, 2, nk - 1), dma(SWEEPS + 1, 2, nk - 1),
         ],
         compiler_params=pltpu.CompilerParams(
             collective_id=0, has_side_effects=True, vmem_limit_bytes=67043328

time: 45.6 us -> 36 us (0.79)
  Pallas kernels: 43.4 us -> 33.8 us
    pallas_call x1, Pallas kernels: 43.4 us -> 33.8 us  [local(): pl.pallas_call(functools.partial(kernel, ni, nk), out_shape=jax.ShapeDtyp...]
where the time goes in v1:
time: 36 us; the launch traced here: 35.8 us
  Pallas kernels  33.8 us (94%)
  local copies, waits for them, and re-layouts  2.06 us (6%)
    pallas_call x1, Pallas kernels, local(): pl.pallas_call(functools.partial(kernel, ni, nk), out_shape=jax.ShapeDtyp...  33.8 us
    unnamed x1, local copies, waits for them, and re-layouts  2.06 us

profile of v1, /device:TPU:31, one launch (start us, length us, event | category | flops | bytes accessed | tf_op | source)
XLA Modules:
  0.0 35.8 jit_solution(15089841216487213742)
XLA Ops:
  0.0 33.8 %shard_map.73 = f32[16,2,3,8,256]{4,3,2,1,0:T(8,128)} custom-call(f32[16,2,3,8,256]{4,3,2,1,0:T(8,128)} %field.1, f32[16,2,3,8,256]{4,3,2,1,0:T(8,128)} %source.1, s32[16,8,256]{2,1,0:T(8,128)} %classes.1, s32[16,8,256]{2,1,0:T(8,128)} %boundary.1, f32[16]{0:T(128)} %conductance.1, f32[3]{0:T(128)} %angles.1, f32[3]{0:T(128)} %strengths.1), custom_call_target="tpu_custom_call" | custom-call | tf_op jit(solution)/shard_map/pallas_call | solution.py:431
  33.8 2.1 %copy.9 = f32[16,2,3,8,256]{4,3,2,1,0:T(8,128)} copy(f32[16,2,3,8,256]{4,3,2,1,0:T(8,128)} %shard_map.73) | data formatting | bytes 1572864

commit v2 on v1

--- a/solution.py
+++ b/solution.py
@@ -430,7 +430,7 @@
     scalars = pl.BlockSpec(memory_space=pltpu.SMEM)
     return pl.pallas_call(
         functools.partial(kernel, ni, nk),
-        out_shape=jax.ShapeDtypeStruct(block, jnp.float32),
+        out_shape=pltpu.VMEM(block, jnp.float32),
         in_specs=[whole] * 4 + [scalars] * 3,
         out_specs=pl.BlockSpec(memory_space=pltpu.VMEM),
         scratch_shapes=[
@@ -446,7 +446,7 @@
             dma(SWEEPS + 1, 2, nk - 1), dma(SWEEPS + 1, 2, nk - 1),
         ],
         compiler_params=pltpu.CompilerParams(
-            collective_id=0, has_side_effects=True, vmem_limit_bytes=67043328
+            collective_id=0, has_side_effects=True, vmem_limit_bytes=56 * 1024 * 1024
         ),
     )(field, source, classes, boundary, conductance, angles, strengths)
 

time: 36 us -> 33.9 us (0.942)
  local copies, waits for them, and re-layouts: 2.06 us -> 0.88 us
  Pallas kernels: 33.8 us -> 32.9 us
    unnamed x1, local copies, waits for them, and re-layouts: 2.06 us -> 0.88 us
    pallas_call x1, Pallas kernels: 33.8 us -> 32.9 us  [local(): pl.pallas_call(functools.partial(kernel, ni, nk), out_shape=pltpu.VMEM(bl...]
where the time goes in v2:
time: 33.9 us; the launch traced here: 33.8 us
  Pallas kernels  32.9 us (97%)
  local copies, waits for them, and re-layouts  0.88 us (3%)
    pallas_call x1, Pallas kernels, local(): pl.pallas_call(functools.partial(kernel, ni, nk), out_shape=pltpu.VMEM(bl...  32.9 us
    unnamed x1, local copies, waits for them, and re-layouts  0.88 us

profile of v2, /device:TPU:31, one launch (start us, length us, event | category | flops | bytes accessed | tf_op | source)
XLA Modules:
  0.0 33.8 jit_solution(16811334362444286253)
XLA Ops:
  0.0 32.9 %shard_map.73 = f32[16,2,3,8,256]{4,3,2,1,0:T(8,128)S(1)} custom-call(f32[16,2,3,8,256]{4,3,2,1,0:T(8,128)} %field.1, f32[16,2,3,8,256]{4,3,2,1,0:T(8,128)} %source.1, s32[16,8,256]{2,1,0:T(8,128)} %classes.1, s32[16,8,256]{2,1,0:T(8,128)} %boundary.1, f32[16]{0:T(128)} %conductance.1, f32[3]{0:T(128)} %angles.1, f32[3]{0:T(128)} %strengths.1), custom_call_target="tpu_custom_call" | custom-call | tf_op jit(solution)/shard_map/pallas_call | solution.py:431
  32.9 0.9 %copy.9 = f32[16,2,3,8,256]{4,3,2,1,0:T(8,128)} copy(f32[16,2,3,8,256]{4,3,2,1,0:T(8,128)S(1)} %shard_map.73) | data formatting | bytes 1572864

commit v3 on v2

--- a/solution.py
+++ b/solution.py
@@ -68,13 +68,24 @@
     cur, src, cls, bnd, piv, vec_v, vec_u, rhs, sol,
     ends, coef_r, coef_c,
     halo_out, halo_in, chain_out, chain_in, edge_out, edge_in,
+    whole_out, whole_in,
+    diag, mate_diag_out, mate_diag, mate_piv, mate_v, mate_u, mate_out, mate_in,
     load_sem, halo_send, halo_recv, chain_send, chain_recv, edge_send, edge_recv,
+    diag_send, diag_recv, mate_send, mate_recv, whole_send, whole_recv,
 ):
     i = lax.axis_index("xy")
     k = lax.axis_index("gz")
     depth, _, comps, rows, lanes = cur.shape
     per = depth // CHUNKS
     last = depth - 1
+    middle = ni // 2
+    mate = ni - 1 - i
+
+    def crossing(side):
+        return i + side == middle
+
+    paired = crossing(0) | crossing(1)
+    direct = lax.rem(i, 2) == 0
 
     loads = [
         pltpu.make_async_copy(a, b, load_sem.at[n])
@@ -86,7 +97,8 @@
     barrier = pltpu.get_barrier_semaphore()
     neighbours = [(i > 0, {"xy": i - 1}), (i < ni - 1, {"xy": i + 1})]
     for far in range(1, nk):
-        neighbours += [(k >= far, {"gz": k - far}), (k < nk - far, {"gz": k + far})]
+        for there, target in ((k >= far, k - far), (k < nk - far, k + far)):
+            neighbours += [(there, {"gz": target}), (there & paired, {"xy": mate, "gz": target})]
     for there, target in neighbours:
         @pl.when(there)
         def _():
@@ -98,6 +110,10 @@
             for n in range(SWEEPS):
                 halo_in[n, side] = jnp.zeros(halo_in.shape[2:], jnp.float32)
 
+        @pl.when(crossing(side))
+        def _():
+            halo_in[SWEEPS - 1, side] = jnp.zeros(halo_in.shape[2:], jnp.float32)
+
     for way, place in ((0, k), (1, nk - 1 - k)):
         @pl.when(place == 0)
         def _():
@@ -107,43 +123,58 @@
         for far in range(1, nk):
             @pl.when(place < far)
             def _():
-                for n in range(SWEEPS + 1):
+                for n in range(SWEEPS + 2):
                     edge_in[n, way, far - 1] = jnp.zeros(edge_in.shape[3:], jnp.float32)
+                whole_in[1, way, far - 1] = jnp.zeros(whole_in.shape[3:], jnp.float32)
+
+            @pl.when(place <= far)
+            def _():
+                whole_in[0, way, far - 1] = jnp.zeros(whole_in.shape[3:], jnp.float32)
 
     turn = rotation(angles)
 
-    def halo_copy(number, side, chunk):
+    def halo_copy(number, slot, side, chunk):
         part = pl.ds(chunk * per, per)
         return pltpu.make_async_remote_copy(
             src_ref=halo_out.at[number, side, part],
-            dst_ref=halo_in.at[number, 1 - side, part],
+            dst_ref=halo_in.at[slot, 1 - side, part],
             send_sem=halo_send.at[number, side, chunk],
-            recv_sem=halo_recv.at[number, 1 - side, chunk],
+            recv_sem=halo_recv.at[slot, 1 - side, chunk],
             device_id={"xy": i + 2 * side - 1},
             device_id_type=MESH,
         )
 
     sides = ((0, i > 0), (1, i < ni - 1))
 
+    def slot_of(number, side):
+        if number < SWEEPS - 1:
+            return number
+        return number + crossing(side).astype(jnp.int32)
+
     def send_halo(number, chunk):
         for side, there in sides:
             @pl.when(there)
             def _():
-                halo_copy(number, side, chunk).start()
+                halo_copy(number, slot_of(number, side), side, chunk).start()
+
+    def wait_slot(number, slot, side):
+        for chunk in range(CHUNKS):
+            halo_copy(number, slot, 1 - side, chunk).wait_recv()
 
     def wait_halo(number):
         for side, there in sides:
-            @pl.when(there)
-            def _():
-                for chunk in range(CHUNKS):
-                    halo_copy(number, 1 - side, chunk).wait_recv()
+            late = crossing(side) if number == SWEEPS - 1 else False
+
+            @pl.when(there & jnp.logical_not(late))
+            def _():
+                wait_slot(number, number, side)
 
     def finish_halo(number):
         for side, there in sides:
             @pl.when(there)
             def _():
                 for chunk in range(CHUNKS):
-                    halo_copy(number, side, chunk).wait_send()
+                    halo_copy(number, slot_of(number, side), side, chunk).wait_send()
 
     def place_of(way):
         return jnp.where(way == 0, k, nk - 1 - k)
@@ -211,6 +242,64 @@
                 def _():
                     edge_copy(stage, way, far).wait_send()
 
+    def whole_copy(kind, way, far):
+        return pltpu.make_async_remote_copy(
+            src_ref=whole_out.at[kind, way],
+            dst_ref=whole_in.at[kind, way, far - 1],
+            send_sem=whole_send.at[kind, way, far - 1],
+            recv_sem=whole_recv.at[kind, way, far - 1],
+            device_id={"gz": k + far * (1 - 2 * way)},
+            device_id_type=MESH,
+        )
+
+    def sends_whole(kind, way, far):
+        place = place_of(way)
+        return (place < nk - far) & (place > 0) if kind == 0 else place < nk - far
+
+    def send_whole(kind, way, values):
+        for comp in range(comps):
+            put(whole_out, values[comp], kind, way, comp)
+        for far in range(nk - 1, 0, -1):
+            @pl.when(sends_whole(kind, way, far))
+            def _():
+                whole_copy(kind, way, far).start()
+
+    def wait_whole():
+        for way in range(2):
+            for far in range(1, nk):
+                for kind in range(2):
+                    @pl.when(place_of(way) >= far + 1 - kind)
+                    def _():
+                        whole_copy(kind, way, far).wait_recv()
+
+    def finish_whole():
+        for way in range(2):
+            for far in range(1, nk):
+                for kind in range(2):
+                    @pl.when(sends_whole(kind, way, far))
+                    def _():
+                        whole_copy(kind, way, far).wait_send()
+
+    def diag_copy():
+        return pltpu.make_async_remote_copy(
+            src_ref=mate_diag_out,
+            dst_ref=mate_diag,
+            send_sem=diag_send,
+            recv_sem=diag_recv,
+            device_id={"xy": mate},
+            device_id_type=MESH,
+        )
+
+    def mate_copy(way, far):
+        return pltpu.make_async_remote_copy(
+            src_ref=mate_out,
+            dst_ref=mate_in.at[way, far - 1],
+            send_sem=mate_send.at[way, far - 1],
+            recv_sem=mate_recv.at[way, far - 1],
+            device_id={"xy": mate, "gz": k + far * (1 - 2 * way)},
+            device_id_type=MESH,
+        )
+
     loads[0].wait()
     for z in range(depth):
         for part in range(2):
@@ -223,6 +312,7 @@
     for z in range(depth):
         sigma = look_up(conductance, conductance.shape[0], cls[z])
         real = (2.0 + 4.0 * COUPLING) + PENALTY * bnd[z].astype(jnp.float32)
+        put(diag, (real, sigma), z)
         for comp in range(comps):
             diagonal = (real, sigma * strengths[comp])
             if z:
@@ -254,6 +344,78 @@
     pl.semaphore_wait(barrier, sum(there.astype(jnp.int32) for there, _ in neighbours))
     for chunk in range(CHUNKS):
         send_halo(0, chunk)
+    for side in range(2):
+        @pl.when(crossing(side))
+        def _():
+            row = side * (rows - 1)
+            for z in range(depth):
+                mate_diag_out[z] = diag[z, :, row:row + 1]
+            diag_copy().start()
+
+    def mate_columns():
+        diag_copy().wait_recv()
+        for z in range(depth):
+            real, sigma = get(mate_diag, z)
+            for comp in range(comps):
+                diagonal = (real, sigma * strengths[comp])
+                if z:
+                    before = get(mate_piv, z - 1, comp)
+                    diagonal = (diagonal[0] - before[0], diagonal[1] - before[1])
+                put(mate_piv, inverse(diagonal), z, comp)
+                if z == 1:
+                    put(mate_v, before, z, comp)
+                elif z > 1:
+                    put(mate_v, mul(before, get(mate_v, z - 1, comp)), z, comp)
+        for comp in range(comps):
+            pivot = get(mate_piv, last, comp)
+            column_v, column_u = mul(pivot, get(mate_v, last, comp)), pivot
+            put(mate_v, column_v, last, comp)
+            put(mate_u, column_u, last, comp)
+            for z in range(last - 1, -1, -1):
+                pivot = get(mate_piv, z, comp)
+                column_u = mul(pivot, column_u)
+                put(mate_u, column_u, z, comp)
+                if z:
+                    column_v = mul(pivot, add(get(mate_v, z, comp), column_v))
+                else:
+                    column_v = mul(pivot, (1.0 + column_v[0], column_v[1]))
+                put(mate_v, column_v, z, comp)
+
+    def send_to_mates(side):
+        row = side * (rows - 1)
+        for comp in range(comps):
+            for end, column in enumerate((mate_v, mate_u)):
+                total = None
+                for z in range(depth):
+                    ours = get(sol, z, comp)
+                    term = mul(
+                        get(column, z, comp), (ours[0][row:row + 1], ours[1][row:row + 1])
+                    )
+                    total = term if total is None else add(total, term)
+                put(mate_out, (COUPLING * total[0], COUPLING * total[1]), comp, end)
+        for way in range(2):
+            for far in range(nk - 1, 0, -1):
+                @pl.when(place_of(way) < nk - far)
+                def _():
+                    mate_copy(way, far).start()
+
+    def add_from_mates(stage, side):
+        for way in range(2):
+            for far in range(1, nk):
+                @pl.when(place_of(way) >= far)
+                def _():
+                    mate_copy(way, far).wait_recv()
+                    for comp in range(comps):
+                        near = get(mate_in, way, far - 1, comp, way)
+                        beyond = get(mate_in, way, far - 1, comp, 1 - way)
+                        link = get(edge_in, SWEEPS + 1, way, far - 1, comp)
+                        link = (link[0][side:side + 1], link[1][side:side + 1])
+                        extra = add(beyond, mul(link, near))
+                        for part in range(2):
+                            edge_in[stage, way, far - 1, comp, part, side:side + 1] = (
+                                edge_in[stage, way, far - 1, comp, part, side:side + 1]
+                                + extra[part]
+                            )
 
     def coefficient_step(way, comp, arrived):
         near, far = get(ends, way, comp), get(ends, 1 - way, comp)
@@ -267,6 +429,10 @@
     def relay_coefficients(way):
         relay(0, way, coefficient_step)
         send_edges(0, way, [get(coef_c, way, comp) for comp in range(comps)])
+
+        @pl.when(paired)
+        def _():
+            send_edges(SWEEPS + 1, way, [get(coef_r, way, comp) for comp in range(comps)])
 
     def local_forcing(way, comp):
         near = get(sol, last * way, comp)
@@ -303,14 +469,14 @@
             forward(z, [get(rhs, z, comp) for comp in range(comps)])
         backward()
 
-    def with_halo(number):
+    def with_halo(above, below):
         for z in range(depth):
             added = []
             for part in range(2):
                 outer = jnp.where(
                     sublane == 0,
-                    halo_in[number, 0, z, part],
-                    jnp.where(sublane == rows - 1, halo_in[number, 1, z, part], 0.0),
+                    halo_in[above, 0, z, part],
+                    jnp.where(sublane == rows - 1, halo_in[below, 1, z, part], 0.0),
                 )
                 added.append(turned_back(COUPLING * outer))
             forward(z, [
@@ -340,6 +506,25 @@
         relay_coefficients(near_way)
 
     loads[3].wait()
+    ender = place_of(far_way) == nk - 1
+
+    def combine_whole(stage):
+        for way in range(2):
+            for comp in range(comps):
+                total = get(whole_in, 1, way, nk - 2, comp)
+                for far in range(nk - 2, 0, -1):
+                    passed = mul(get(whole_in, 0, way, far - 1, comp), total)
+                    total = add(get(whole_in, 1, way, far - 1, comp), passed)
+                put(chain_in, total, stage, way, comp)
+
+    def with_mate_halo(number):
+        for side in range(2):
+            @pl.when(crossing(side))
+            def _():
+                wait_slot(number, SWEEPS, side)
+
+        with_halo(slot_of(number, 0), slot_of(number, 1))
+
     for number in range(SWEEPS):
         stage = number + 1
         without_halo()
@@ -348,18 +533,69 @@
             def _():
                 relay_coefficients(near_way)
 
-        relay(stage, near_way, forcing_step)
+            relay(stage, near_way, forcing_step)
+        else:
+            @pl.when(direct)
+            def _():
+                for way in range(2):
+                    send_whole(1, way, [local_forcing(way, comp) for comp in range(comps)])
+
+            @pl.when(jnp.logical_not(direct))
+            def _():
+                relay(stage, near_way, forcing_step)
+
         wait_halo(number)
-        with_halo(number)
+        with_halo(number, number)
         send_forcing_edges(stage, near_way)
         if number == 0:
+            @pl.when(paired & ender)
+            def _():
+                mate_columns()
+
             relay_coefficients(far_way)
-        send_forcing_edges(stage, far_way)
-        relay(stage, far_way, forcing_step)
-
-        if number == 0:
+            send_forcing_edges(stage, far_way)
+            relay(stage, far_way, forcing_step)
+
+            @pl.when(direct)
+            def _():
+                for way in range(2):
+                    send_whole(0, way, [get(coef_c, way, comp) for comp in range(comps)])
+
+            @pl.when(paired & jnp.logical_not(ender))
+            def _():
+                mate_columns()
+
             wait_edges(0)
+        else:
+            send_forcing_edges(stage, far_way)
+
+            @pl.when(paired & ender)
+            def _():
+                with_mate_halo(number)
+
+            @pl.when(direct)
+            def _():
+                wait_whole()
+                combine_whole(stage)
+
+            @pl.when(jnp.logical_not(direct))
+            def _():
+                relay(stage, far_way, forcing_step)
+
+            @pl.when(paired & jnp.logical_not(ender))
+            def _():
+                with_mate_halo(number)
+
         wait_edges(stage)
+        if stage == SWEEPS:
+            @pl.when(paired)
+            def _():
+                wait_edges(SWEEPS + 1)
+                for side in range(2):
+                    @pl.when(crossing(side))
+                    def _():
+                        add_from_mates(stage, side)
+
         first_in, last_in = [], []
         for comp in range(comps):
             arrived, leaving = [], []
@@ -396,6 +632,8 @@
                         mul(get(vec_u, z, comp), last_in[comp]),
                     )
                     solved.append(add(get(sol, z, comp), value))
+                    if stage == SWEEPS - 1:
+                        put(sol, solved[comp], z, comp)
                 for part in range(2):
                     for c in range(comps):
                         value = (
@@ -411,12 +649,36 @@
                             halo_out[stage, 1, z, part, c] = value[rows - 1:]
             if stage < SWEEPS:
                 send_halo(stage, chunk)
+        if stage == SWEEPS - 1:
+            for side in range(2):
+                @pl.when(crossing(side))
+                def _():
+                    send_to_mates(side)
 
     for number in range(SWEEPS):
         finish_halo(number)
     for stage in range(SWEEPS + 1):
-        finish_chain(stage)
+        if stage < SWEEPS:
+            finish_chain(stage)
         finish_edges(stage)
+
+    @pl.when(direct)
+    def _():
+        finish_whole()
+
+    @pl.when(jnp.logical_not(direct))
+    def _():
+        finish_chain(SWEEPS)
+
+    @pl.when(paired)
+    def _():
+        finish_edges(SWEEPS + 1)
+        diag_copy().wait_send()
+        for way in range(2):
+            for far in range(1, nk):
+                @pl.when(place_of(way) < nk - far)
+                def _():
+                    mate_copy(way, far).wait_send()
 
 
 def local(ni, nk, field, source, classes, boundary, conductance, angles, strengths):
@@ -424,6 +686,7 @@
     block = (depth, 2, comps, rows, lanes)
     lines = (depth, comps, 2, rows, lanes)
     ends = (2, comps, 2, rows, lanes)
+    row_lines = (depth, comps, 2, 1, lanes)
     vmem = lambda *shape: pltpu.VMEM(shape, jnp.float32)
     dma = lambda *shape: pltpu.SemaphoreType.DMA(shape)
     whole = pl.BlockSpec(memory_space=pltpu.HBM)
@@ -438,12 +701,18 @@
             pltpu.VMEM(classes.shape, jnp.int32), pltpu.VMEM(boundary.shape, jnp.int32),
             vmem(*lines), vmem(*lines), vmem(*lines), vmem(*lines), vmem(*lines),
             vmem(*ends), vmem(*ends), vmem(*ends),
-            vmem(SWEEPS, 2, depth, 2, comps, 1, lanes), vmem(SWEEPS, 2, depth, 2, comps, 1, lanes),
+            vmem(SWEEPS, 2, depth, 2, comps, 1, lanes), vmem(SWEEPS + 1, 2, depth, 2, comps, 1, lanes),
             vmem(SWEEPS + 1, *ends), vmem(SWEEPS + 1, *ends),
-            vmem(SWEEPS + 1, 2, comps, 2, 2, lanes), vmem(SWEEPS + 1, 2, nk - 1, comps, 2, 2, lanes),
-            dma(4), dma(SWEEPS, 2, CHUNKS), dma(SWEEPS, 2, CHUNKS),
+            vmem(SWEEPS + 2, 2, comps, 2, 2, lanes), vmem(SWEEPS + 2, 2, nk - 1, comps, 2, 2, lanes),
+            vmem(2, *ends), vmem(2, 2, nk - 1, *ends[1:]),
+            vmem(depth, 2, rows, lanes), vmem(depth, 2, 1, lanes), vmem(depth, 2, 1, lanes),
+            vmem(*row_lines), vmem(*row_lines), vmem(*row_lines),
+            vmem(comps, 2, 2, 1, lanes), vmem(2, nk - 1, comps, 2, 2, 1, lanes),
+            dma(4), dma(SWEEPS, 2, CHUNKS), dma(SWEEPS + 1, 2, CHUNKS),
             dma(SWEEPS + 1, 2, comps), dma(SWEEPS + 1, 2, comps),
-            dma(SWEEPS + 1, 2, nk - 1), dma(SWEEPS + 1, 2, nk - 1),
+            dma(SWEEPS + 2, 2, nk - 1), dma(SWEEPS + 2, 2, nk - 1),
+            pltpu.SemaphoreType.DMA, pltpu.SemaphoreType.DMA, dma(2, nk - 1), dma(2, nk - 1),
+            dma(2, 2, nk - 1), dma(2, 2, nk - 1),
         ],
         compiler_params=pltpu.CompilerParams(
             collective_id=0, has_side_effects=True, vmem_limit_bytes=56 * 1024 * 1024

time: 33.9 us -> 33.1 us (0.976)
  Pallas kernels: 32.9 us -> 32.1 us
    pallas_call x1, Pallas kernels: 32.9 us -> 32.1 us  [local(): pl.pallas_call(functools.partial(kernel, ni, nk), out_shape=pltpu.VMEM(bl...]
where the time goes in v3:
time: 33.1 us; the launch traced here: 33 us
  Pallas kernels  32.1 us (97%)
  local copies, waits for them, and re-layouts  0.88 us (3%)
    pallas_call x1, Pallas kernels, local(): pl.pallas_call(functools.partial(kernel, ni, nk), out_shape=pltpu.VMEM(bl...  32.1 us
    unnamed x1, local copies, waits for them, and re-layouts  0.88 us

profile of v3, /device:TPU:31, one launch (start us, length us, event | category | flops | bytes accessed | tf_op | source)
XLA Modules:
  0.0 33.0 jit_solution(16043852598160019750)
XLA Ops:
  0.0 32.1 %shard_map.73 = f32[16,2,3,8,256]{4,3,2,1,0:T(8,128)S(1)} custom-call(f32[16,2,3,8,256]{4,3,2,1,0:T(8,128)} %field.1, f32[16,2,3,8,256]{4,3,2,1,0:T(8,128)} %source.1, s32[16,8,256]{2,1,0:T(8,128)} %classes.1, s32[16,8,256]{2,1,0:T(8,128)} %boundary.1, f32[16]{0:T(128)} %conductance.1, f32[3]{0:T(128)} %angles.1, f32[3]{0:T(128)} %strengths.1), custom_call_target="tpu_custom_call" | custom-call | tf_op jit(solution)/shard_map/pallas_call | solution.py:694
  32.1 0.9 %copy.9 = f32[16,2,3,8,256]{4,3,2,1,0:T(8,128)} copy(f32[16,2,3,8,256]{4,3,2,1,0:T(8,128)S(1)} %shard_map.73) | data formatting | bytes 1572864

commit v4 on v3

--- a/solution.py
+++ b/solution.py
@@ -63,8 +63,9 @@
 
 def kernel(
     ni, nk,
-    field, source, classes, boundary, conductance, angles, strengths,
+    field, source, classes, boundary, conductance_hbm, angles_hbm, strengths_hbm,
     out,
+    conductance, angles, strengths,
     cur, src, cls, bnd, piv, vec_v, vec_u, rhs, sol,
     ends, coef_r, coef_c,
     halo_out, halo_in, chain_out, chain_in, edge_out, edge_in,
@@ -87,13 +88,6 @@
     paired = crossing(0) | crossing(1)
     direct = lax.rem(i, 2) == 0
 
-    loads = [
-        pltpu.make_async_copy(a, b, load_sem.at[n])
-        for n, (a, b) in enumerate(((field, cur), (classes, cls), (boundary, bnd), (source, src)))
-    ]
-    for copy in loads:
-        copy.start()
-
     barrier = pltpu.get_barrier_semaphore()
     neighbours = [(i > 0, {"xy": i - 1}), (i < ni - 1, {"xy": i + 1})]
     for far in range(1, nk):
@@ -104,6 +98,16 @@
         def _():
             pl.semaphore_signal(barrier, inc=1, device_id=target, device_id_type=MESH)
 
+    loads = [
+        pltpu.make_async_copy(a, b, load_sem.at[n])
+        for n, (a, b) in enumerate((
+            (field, cur), (classes, cls), (boundary, bnd), (source, src),
+            (conductance_hbm, conductance), (angles_hbm, angles), (strengths_hbm, strengths),
+        ))
+    ]
+    for copy in loads:
+        copy.start()
+
     for side, alone in ((0, i == 0), (1, i == ni - 1)):
         @pl.when(alone)
         def _():
@@ -125,13 +129,12 @@
             def _():
                 for n in range(SWEEPS + 2):
                     edge_in[n, way, far - 1] = jnp.zeros(edge_in.shape[3:], jnp.float32)
-                whole_in[1, way, far - 1] = jnp.zeros(whole_in.shape[3:], jnp.float32)
+                for n in range(1, SWEEPS + 1):
+                    whole_in[n, way, far - 1] = jnp.zeros(whole_in.shape[3:], jnp.float32)
 
             @pl.when(place <= far)
             def _():
                 whole_in[0, way, far - 1] = jnp.zeros(whole_in.shape[3:], jnp.float32)
-
-    turn = rotation(angles)
 
     def halo_copy(number, slot, side, chunk):
         part = pl.ds(chunk * per, per)
@@ -264,18 +267,17 @@
             def _():
                 whole_copy(kind, way, far).start()
 
-    def wait_whole():
+    def wait_whole(kind):
         for way in range(2):
             for far in range(1, nk):
-                for kind in range(2):
-                    @pl.when(place_of(way) >= far + 1 - kind)
-                    def _():
-                        whole_copy(kind, way, far).wait_recv()
+                @pl.when(place_of(way) >= (far if kind else far + 1))
+                def _():
+                    whole_copy(kind, way, far).wait_recv()
 
     def finish_whole():
         for way in range(2):
             for far in range(1, nk):
-                for kind in range(2):
+                for kind in (0, SWEEPS):
                     @pl.when(sends_whole(kind, way, far))
                     def _():
                         whole_copy(kind, way, far).wait_send()
@@ -307,8 +309,8 @@
             halo_out[0, 0, z, part] = here[:, :1]
             halo_out[0, 1, z, part] = here[:, rows - 1:]
 
-    loads[1].wait()
-    loads[2].wait()
+    for n in (1, 2, 4, 6):
+        loads[n].wait()
     for z in range(depth):
         sigma = look_up(conductance, conductance.shape[0], cls[z])
         real = (2.0 + 4.0 * COUPLING) + PENALTY * bnd[z].astype(jnp.float32)
@@ -506,15 +508,17 @@
         relay_coefficients(near_way)
 
     loads[3].wait()
+    loads[5].wait()
+    turn = rotation(angles)
     ender = place_of(far_way) == nk - 1
 
     def combine_whole(stage):
         for way in range(2):
             for comp in range(comps):
-                total = get(whole_in, 1, way, nk - 2, comp)
+                total = get(whole_in, stage, way, nk - 2, comp)
                 for far in range(nk - 2, 0, -1):
                     passed = mul(get(whole_in, 0, way, far - 1, comp), total)
-                    total = add(get(whole_in, 1, way, far - 1, comp), passed)
+                    total = add(get(whole_in, stage, way, far - 1, comp), passed)
                 put(chain_in, total, stage, way, comp)
 
     def with_mate_halo(number):
@@ -525,6 +529,11 @@
 
         with_halo(slot_of(number, 0), slot_of(number, 1))
 
+    def far_first():
+        relay_coefficients(far_way)
+        relay(1, far_way, forcing_step)
+
+    early = paired & jnp.logical_not(ender)
     for number in range(SWEEPS):
         stage = number + 1
         without_halo()
@@ -534,11 +543,15 @@
                 relay_coefficients(near_way)
 
             relay(stage, near_way, forcing_step)
+
+            @pl.when(early)
+            def _():
+                far_first()
         else:
             @pl.when(direct)
             def _():
                 for way in range(2):
-                    send_whole(1, way, [local_forcing(way, comp) for comp in range(comps)])
+                    send_whole(stage, way, [local_forcing(way, comp) for comp in range(comps)])
 
             @pl.when(jnp.logical_not(direct))
             def _():
@@ -552,9 +565,11 @@
             def _():
                 mate_columns()
 
-            relay_coefficients(far_way)
+            @pl.when(jnp.logical_not(early))
+            def _():
+                far_first()
+
             send_forcing_edges(stage, far_way)
-            relay(stage, far_way, forcing_step)
 
             @pl.when(direct)
             def _():
@@ -575,7 +590,8 @@
 
             @pl.when(direct)
             def _():
-                wait_whole()
+                wait_whole(0)
+                wait_whole(stage)
                 combine_whole(stage)
 
             @pl.when(jnp.logical_not(direct))
@@ -658,9 +674,9 @@
     for number in range(SWEEPS):
         finish_halo(number)
     for stage in range(SWEEPS + 1):
-        if stage < SWEEPS:
-            finish_chain(stage)
         finish_edges(stage)
+    for stage in range(SWEEPS):
+        finish_chain(stage)
 
     @pl.when(direct)
     def _():
@@ -690,13 +706,13 @@
     vmem = lambda *shape: pltpu.VMEM(shape, jnp.float32)
     dma = lambda *shape: pltpu.SemaphoreType.DMA(shape)
     whole = pl.BlockSpec(memory_space=pltpu.HBM)
-    scalars = pl.BlockSpec(memory_space=pltpu.SMEM)
     return pl.pallas_call(
         functools.partial(kernel, ni, nk),
         out_shape=pltpu.VMEM(block, jnp.float32),
-        in_specs=[whole] * 4 + [scalars] * 3,
+        in_specs=[whole] * 7,
         out_specs=pl.BlockSpec(memory_space=pltpu.VMEM),
         scratch_shapes=[
+            *[pltpu.SMEM(v.shape, jnp.float32) for v in (conductance, angles, strengths)],
             vmem(*block), vmem(*block),
             pltpu.VMEM(classes.shape, jnp.int32), pltpu.VMEM(boundary.shape, jnp.int32),
             vmem(*lines), vmem(*lines), vmem(*lines), vmem(*lines), vmem(*lines),
@@ -704,15 +720,15 @@
             vmem(SWEEPS, 2, depth, 2, comps, 1, lanes), vmem(SWEEPS + 1, 2, depth, 2, comps, 1, lanes),
             vmem(SWEEPS + 1, *ends), vmem(SWEEPS + 1, *ends),
             vmem(SWEEPS + 2, 2, comps, 2, 2, lanes), vmem(SWEEPS + 2, 2, nk - 1, comps, 2, 2, lanes),
-            vmem(2, *ends), vmem(2, 2, nk - 1, *ends[1:]),
+            vmem(SWEEPS + 1, *ends), vmem(SWEEPS + 1, 2, nk - 1, *ends[1:]),
             vmem(depth, 2, rows, lanes), vmem(depth, 2, 1, lanes), vmem(depth, 2, 1, lanes),
             vmem(*row_lines), vmem(*row_lines), vmem(*row_lines),
             vmem(comps, 2, 2, 1, lanes), vmem(2, nk - 1, comps, 2, 2, 1, lanes),
-            dma(4), dma(SWEEPS, 2, CHUNKS), dma(SWEEPS + 1, 2, CHUNKS),
+            dma(7), dma(SWEEPS, 2, CHUNKS), dma(SWEEPS + 1, 2, CHUNKS),
             dma(SWEEPS + 1, 2, comps), dma(SWEEPS + 1, 2, comps),
             dma(SWEEPS + 2, 2, nk - 1), dma(SWEEPS + 2, 2, nk - 1),
             pltpu.SemaphoreType.DMA, pltpu.SemaphoreType.DMA, dma(2, nk - 1), dma(2, nk - 1),
-            dma(2, 2, nk - 1), dma(2, 2, nk - 1),
+            dma(SWEEPS + 1, 2, nk - 1), dma(SWEEPS + 1, 2, nk - 1),
         ],
         compiler_params=pltpu.CompilerParams(
             collective_id=0, has_side_effects=True, vmem_limit_bytes=56 * 1024 * 1024

time: 33.1 us -> 32.5 us (0.982)
  Pallas kernels: 32.1 us -> 31.5 us
    pallas_call x1, Pallas kernels: 32.1 us -> 31.5 us  [local(): pl.pallas_call(functools.partial(kernel, ni, nk), out_shape=pltpu.VMEM(bl...]
where the time goes in v4:
time: 32.5 us; the launch traced here: 32.4 us
  Pallas kernels  31.5 us (97%)
  local copies, waits for them, and re-layouts  0.88 us (3%)
    pallas_call x1, Pallas kernels, local(): pl.pallas_call(functools.partial(kernel, ni, nk), out_shape=pltpu.VMEM(bl...  31.5 us
    unnamed x1, local copies, waits for them, and re-layouts  0.88 us

profile of v4, /device:TPU:31, one launch (start us, length us, event | category | flops | bytes accessed | tf_op | source)
XLA Modules:
  0.0 32.4 jit_solution(330212933852044730)
XLA Ops:
  0.0 31.5 %shard_map.73 = f32[16,2,3,8,256]{4,3,2,1,0:T(8,128)S(1)} custom-call(f32[16,2,3,8,256]{4,3,2,1,0:T(8,128)} %field.1, f32[16,2,3,8,256]{4,3,2,1,0:T(8,128)} %source.1, s32[16,8,256]{2,1,0:T(8,128)} %classes.1, s32[16,8,256]{2,1,0:T(8,128)} %boundary.1, f32[16]{0:T(128)} %conductance_hbm.1, f32[3]{0:T(128)} %angles_hbm.1, f32[3]{0:T(128)} %strengths_hbm.1), custom_call_target="tpu_custom_call" | custom-call | tf_op jit(solution)/shard_map/pallas_call | solution.py:709
  31.5 0.9 %copy.9 = f32[16,2,3,8,256]{4,3,2,1,0:T(8,128)} copy(f32[16,2,3,8,256]{4,3,2,1,0:T(8,128)S(1)} %shard_map.73) | data formatting | bytes 1572864

commit v5 on v4

--- a/solution.py
+++ b/solution.py
@@ -86,7 +86,7 @@
         return i + side == middle
 
     paired = crossing(0) | crossing(1)
-    direct = lax.rem(i, 2) == 0
+    direct = (lax.rem(i, 2) == 0) & jnp.logical_not(paired)
 
     barrier = pltpu.get_barrier_semaphore()
     neighbours = [(i > 0, {"xy": i - 1}), (i < ni - 1, {"xy": i + 1})]

time: 32.5 us -> 31.8 us (0.978)
  Pallas kernels: 31.5 us -> 30.6 us
    pallas_call x1, Pallas kernels: 31.5 us -> 30.6 us  [local(): pl.pallas_call(functools.partial(kernel, ni, nk), out_shape=pltpu.VMEM(bl...]
where the time goes in v5:
time: 31.8 us; the launch traced here: 31.5 us
  Pallas kernels  30.6 us (96%)
  local copies, waits for them, and re-layouts  0.88 us (3%)
    pallas_call x1, Pallas kernels, local(): pl.pallas_call(functools.partial(kernel, ni, nk), out_shape=pltpu.VMEM(bl...  30.6 us
    unnamed x1, local copies, waits for them, and re-layouts  0.88 us

profile of v5, /device:TPU:31, one launch (start us, length us, event | category | flops | bytes accessed | tf_op | source)
XLA Modules:
  0.0 31.5 jit_solution(3975819589991024428)
XLA Ops:
  0.0 30.6 %shard_map.73 = f32[16,2,3,8,256]{4,3,2,1,0:T(8,128)S(1)} custom-call(f32[16,2,3,8,256]{4,3,2,1,0:T(8,128)} %field.1, f32[16,2,3,8,256]{4,3,2,1,0:T(8,128)} %source.1, s32[16,8,256]{2,1,0:T(8,128)} %classes.1, s32[16,8,256]{2,1,0:T(8,128)} %boundary.1, f32[16]{0:T(128)} %conductance_hbm.1, f32[3]{0:T(128)} %angles_hbm.1, f32[3]{0:T(128)} %strengths_hbm.1), custom_call_target="tpu_custom_call" | custom-call | tf_op jit(solution)/shard_map/pallas_call | solution.py:709
  30.7 0.9 %copy.9 = f32[16,2,3,8,256]{4,3,2,1,0:T(8,128)} copy(f32[16,2,3,8,256]{4,3,2,1,0:T(8,128)S(1)} %shard_map.73) | data formatting | bytes 1572864
